TPU v7x, 32 devices: a whole 2x2x4 slice. The times are simulated.
32 devices in a mesh: grp: 2 (over y), seq: 4 (over z), head: 4 (over x, core).
Axes of the slice: x: 2, y: 2, z: 4, core: 2. Of those that a mesh axis runs over, the one named last changes fastest.
Arguments:
- draft_features: bfloat16 [2048, 8192], P(('grp', 'seq'), 'head'), parts along dimension 0, may hold values from -6 to 6
- w_key: bfloat16 [8192, 1024], P(None, 'head'), may hold values from -0.0625 to 0.0625
- w_value: bfloat16 [8192, 1024], P(None, 'head'), may hold values from -0.0625 to 0.0625
- accepted: int32 [256], P(('grp', 'seq')), parts along dimension 0, may hold values from 1 to 8
- owner_group: int32 [256], P(('grp', 'seq')), parts along dimension 0, may hold values from 0 to 3, as said below
- page_slot: int32 [256], P(('grp', 'seq')), parts along dimension 0, may hold values from 0 to 63, as said below
Outputs:
- key_cache: bfloat16 [512, 8, 1024], P(('grp', 'seq'), None, 'head'), parts along dimension 0
- value_cache: bfloat16 [512, 8, 1024], P(('grp', 'seq'), None, 'head'), parts along dimension 0
There are 2 independent parts, one for each index of `grp`. A program takes and returns all parts, laid end to end along the dimension named above; an argument that names none is the same for every part. Nothing has to cross between parts.
Inputs may be any that keep to these rules, and one draw needn't show every extreme that they name: `owner_group`: the requests of one index of seq go to exactly 2 distinct owners, 16 to each; some owner receives 64 requests. `page_slot`: the requests of one owner have distinct slots.
All inputs are finite; a program needn't handle non-finite values.
Results may differ from a plain program's by a relative error of at most 0.001.
Values may be sent and summed in bfloat16 or wider, within the bound.
A program may use at most 64 MiB of HBM per device.

v0:
```python
import jax
import jax.numpy as jnp
from jax import lax
from jax.sharding import PartitionSpec as P


def pair_slots(owner_ids, slot_cap):
    row_count = owner_ids.shape[-1]
    same_owner = owner_ids[..., :, None] == owner_ids[..., None, :]
    before = lax.broadcasted_iota(jnp.int32, (row_count, row_count), 1) < lax.broadcasted_iota(
        jnp.int32, (row_count, row_count), 0
    )
    within = jnp.sum(jnp.where(same_owner & before, 1, 0), axis=-1).astype(jnp.int32)
    return owner_ids * slot_cap + within


def one_hot(labels, columns):
    return (
        labels[:, None] == lax.broadcasted_iota(jnp.int32, (labels.shape[0], columns), 1)
    ).astype(jnp.bfloat16)


def pack_rows(payload, slot_ids, slot_total):
    select = one_hot(slot_ids, slot_total)
    packed = lax.dot_general(
        select, payload, (((0,), (0,)), ((), ())), preferred_element_type=jnp.float32
    )
    return packed.astype(jnp.bfloat16)


def placement(all_owner, all_page, owner_self, req_dev, slot_cap, seq_count):
    slot_total = slot_cap * seq_count
    slot_ids = pair_slots(all_owner.reshape(seq_count, req_dev), slot_cap).reshape(-1)
    source = lax.broadcasted_iota(jnp.int32, (seq_count, req_dev), 0).reshape(-1)
    column = source * slot_cap + slot_ids - all_owner * slot_cap
    target = jnp.where(all_owner == owner_self, all_page, -1)
    to_page = one_hot(target, slot_total)
    from_column = one_hot(column, slot_total)
    placing = lax.dot_general(
        to_page, from_column, (((0,), (0,)), ((), ())), preferred_element_type=jnp.float32
    )
    return placing.astype(jnp.bfloat16)


def local(draft_features, w_key, w_value, accepted, owner_group, page_slot):
    req_dev = accepted.shape[0]
    draft_rows = draft_features.shape[0] // req_dev
    head_cols = w_key.shape[1]
    seq_count = lax.axis_size("seq")
    owner_self = lax.axis_index("seq")
    slot_cap = max(2, 2 * req_dev // seq_count)
    slot_total = slot_cap * seq_count
    send_slots = pair_slots(owner_group, slot_cap)
    live_rows = lax.broadcasted_iota(jnp.int32, (req_dev, draft_rows), 1) < accepted[:, None]
    all_owner, all_page = (
        lax.all_gather(owner_group, "seq", axis=0, tiled=True),
        lax.all_gather(page_slot, "seq", axis=0, tiled=True),
    )
    placing = placement(all_owner, all_page, owner_self, req_dev, slot_cap, seq_count)
    portion = lax.all_gather(draft_features, "head", axis=1, tiled=True)
    key_sum = jnp.dot(portion, w_key, preferred_element_type=jnp.float32)
    value_sum = jnp.dot(portion, w_value, preferred_element_type=jnp.float32)
    key_local = jnp.where(
        live_rows[:, :, None], key_sum.reshape(req_dev, draft_rows, head_cols), 0.0
    )
    value_local = jnp.where(
        live_rows[:, :, None], value_sum.reshape(req_dev, draft_rows, head_cols), 0.0
    )
    key_local = key_local.astype(jnp.bfloat16).reshape(req_dev, draft_rows * head_cols)
    value_local = value_local.astype(jnp.bfloat16).reshape(req_dev, draft_rows * head_cols)
    key_send = pack_rows(key_local, send_slots, slot_total)
    value_send = pack_rows(value_local, send_slots, slot_total)
    key_arrived, value_arrived = (
        lax.all_to_all(key_send, "seq", split_axis=0, concat_axis=0, tiled=True),
        lax.all_to_all(value_send, "seq", split_axis=0, concat_axis=0, tiled=True),
    )
    key_cache = jnp.dot(placing, key_arrived, preferred_element_type=jnp.float32).astype(
        jnp.bfloat16
    )
    value_cache = jnp.dot(placing, value_arrived, preferred_element_type=jnp.float32).astype(
        jnp.bfloat16
    )
    return (
        key_cache.reshape(slot_total, draft_rows, head_cols),
        value_cache.reshape(slot_total, draft_rows, head_cols),
    )


def solution(mesh):
    placed = (
        P(("grp", "seq"), "head"),
        P(None, "head"),
        P(None, "head"),
        P(("grp", "seq")),
        P(("grp", "seq")),
        P(("grp", "seq")),
    )
    return jax.shard_map(
        local,
        mesh=mesh,
        in_specs=placed,
        out_specs=(P(("grp", "seq"), None, "head"), P(("grp", "seq"), None, "head")),
        check_vma=False,
    )
```

profile of v0, /device:TPU:0, one launch (start us, length us, event | category | flops | bytes accessed | tf_op | source)
XLA Modules:
  0.0 84.7 jit_solution(431942104099704447)
XLA Ops:
  7.2 0.0 all-gather.2.cloned.1.call-start
  7.2 0.7 all-gather.2.cloned.1.call-update
  7.9 1.2 %dynamic-slice = u32[1]{0:T(128)} dynamic-slice(u32[32]{0:T(128)} %constant.19, u32[]{:T(128)S(6)} %add.13), dynamic_slice_sizes={1} | dynamic-slice | bytes 12
  9.8 0.9 %dynamic-update-slice = s32[128]{0:T(128)S(1)} dynamic-update-slice(s32[128]{0:T(128)S(1)} %broadcast.31.clone, s32[32]{0:T(128)} %param.10, u32[]{:T(128)} %bitcast) | dynamic-update-slice | bytes 260
  10.7 0.8 dynamic-update-slice.1
  11.5 9.9 %all-reduce.2 = (s32[128]{0:T(128)S(1)}, s32[128]{0:T(128)S(1)}) all-reduce(s32[128]{0:T(128)S(1)} %dynamic-update-slice, s32[128]{0:T(128)S(1)} %dynamic-update-slice.1), channel_id=1, replica_groups=mesh['grp'=2,'seq'=4,'head'=4] {'seq'}, use_global_device_ids=true, to_apply=%add | all-reduce | flops 256 | bytes 2048
  21.4 0.1 eq.66
  21.5 0.1 mul.19
  21.6 0.2 select_reduce_fusion
  21.8 0.1 reduce_sum.21
  21.9 0.7 iota_compare_fusion.4
  22.7 0.1 broadcast_in_dim.53
  22.8 0.9 %select_reduce_fusion.1 = s32[32]{0:T(128)S(1)} fusion(s32[32]{0:T(128)} %param.10), kind=kLoop, calls=%fused_computation.16 | loop fusion | flops 5088 | bytes 256 | tf_op jit(solution)/shard_map/reduce_sum | solution.py:13
  23.7 0.7 multiply_add_fusion
  24.4 22.4 %all-gather.2.cloned.1.call-done = bf16[256,8192]{1,0:T(8,128)(2,1)} async-done(((bf16[256,2048]{1,0:T(8,128)(2,1)}), bf16[256,8192]{1,0:T(8,128)(2,1)}) %all-gather.2.cloned.1.call-update) | async-done | bytes 4194320 | tf_op jit(solution)/shard_map/all_gather | solution.py:60
  46.7 4.7 %fusion.9 = bf16[256,256]{1,0:T(8,128)(2,1)S(1)} fusion(bf16[256,8192]{1,0:T(8,128)(2,1)} %all-gather.2.cloned.1.call-done, bf16[8192,256]{1,0:T(8,128)(2,1)} %param.8), kind=kOutput, calls=%fused_computation.27 | convolution fusion | flops 1073741824 | bytes 8519680 | tf_op jit(solution)/shard_map/dot_general | solution.py:62
  51.5 0.1 reshape.67
  51.5 1.1 %convolution_convert_fusion.1 = bf16[64,2048]{1,0:T(8,128)(2,1)} fusion(pred[32,2048]{1,0:T(8,128)(4,1)S(1)} %bitcast.23, bf16[32,2048]{1,0:T(8,128)(2,1)S(1)} %reshape.67, s32[32]{0:T(128)S(1)} %multiply_add_fusion), kind=kOutput, calls=%fused_computation.1 | convolution fusion | flops 8587264 | bytes 458880 | tf_op jit(solution)/shard_map/dot_general | solution.py:25
  52.6 4.7 %all-to-all-start.1 = ((bf16[4,16,2048]{2,1,0:T(8,128)(2,1)}), bf16[4,16,2048]{2,1,0:T(8,128)(2,1)S(1)}, u32[]{:S(2)}, u32[]{:S(2)}) async-start(bf16[4,16,2048]{2,1,0:T(8,128)(2,1)} %bitcast.3), calls=%async_computation.1 | async-start | bytes 524288 | tf_op jit(solution)/shard_map/all_to_all | solution.py:75
  57.2 4.7 %fusion.8 = bf16[256,256]{1,0:T(8,128)(2,1)S(1)} fusion(bf16[256,8192]{1,0:T(8,128)(2,1)} %all-gather.2.cloned.1.call-done, bf16[8192,256]{1,0:T(8,128)(2,1)} %param.7), kind=kOutput, calls=%fused_computation.26 | convolution fusion | flops 1073741824 | bytes 8519680 | tf_op jit(solution)/shard_map/dot_general | solution.py:61
  62.0 0.1 reshape.65
  62.0 1.1 %convolution_convert_fusion.3 = bf16[64,2048]{1,0:T(8,128)(2,1)} fusion(pred[32,2048]{1,0:T(8,128)(4,1)S(1)} %bitcast.24, bf16[32,2048]{1,0:T(8,128)(2,1)S(1)} %reshape.65, s32[32]{0:T(128)S(1)} %multiply_add_fusion), kind=kOutput, calls=%fused_computation.3 | convolution fusion | flops 8587264 | bytes 458880 | tf_op jit(solution)/shard_map/dot_general | solution.py:25
  63.1 3.5 %all-to-all-done.1 = bf16[4,16,2048]{2,1,0:T(8,128)(2,1)S(1)} async-done(((bf16[4,16,2048]{2,1,0:T(8,128)(2,1)}), bf16[4,16,2048]{2,1,0:T(8,128)(2,1)S(1)}, u32[]{:S(2)}, u32[]{:S(2)}) %all-to-all-start.1) | async-done | bytes 262176 | tf_op jit(solution)/shard_map/all_to_all | solution.py:75
  66.6 3.4 %all-to-all-start = ((bf16[4,16,2048]{2,1,0:T(8,128)(2,1)}), bf16[4,16,2048]{2,1,0:T(8,128)(2,1)S(1)}, u32[]{:S(2)}, u32[]{:S(2)}) async-start(bf16[4,16,2048]{2,1,0:T(8,128)(2,1)} %bitcast.1), calls=%async_computation | async-start | bytes 524288 | tf_op jit(solution)/shard_map/all_to_all | solution.py:74
  70.0 0.3 convolution_convert_fusion.4
  70.2 0.2 convolution_convert_fusion
  70.5 0.8 copy.10
  71.2 5.7 %all-to-all-done = bf16[4,16,2048]{2,1,0:T(8,128)(2,1)S(1)} async-done(((bf16[4,16,2048]{2,1,0:T(8,128)(2,1)}), bf16[4,16,2048]{2,1,0:T(8,128)(2,1)S(1)}, u32[]{:S(2)}, u32[]{:S(2)}) %all-to-all-start) | async-done | bytes 262176 | tf_op jit(solution)/shard_map/all_to_all | solution.py:74
  76.9 0.2 convolution_convert_fusion.2
  77.1 0.8 copy.9
  (6 shorter events, 0.1 us)
Async XLA Ops:
  7.2 39.6 %all-gather.2.cloned.1.call-start = ((), (), s32[]{:S(2)}) async-start(), calls=%async_computation.2 | async-start | bytes 5242880 | tf_op jit(solution)/shard_map/all_gather | solution.py:60
  52.6 14.0 %all-to-all-start.1 = ((bf16[4,16,2048]{2,1,0:T(8,128)(2,1)}), bf16[4,16,2048]{2,1,0:T(8,128)(2,1)S(1)}, u32[]{:S(2)}, u32[]{:S(2)}) async-start(bf16[4,16,2048]{2,1,0:T(8,128)(2,1)} %bitcast.3), calls=%async_computation.1 | async-start | bytes 524288 | tf_op jit(solution)/shard_map/all_to_all | solution.py:75
  66.6 10.3 %all-to-all-start = ((bf16[4,16,2048]{2,1,0:T(8,128)(2,1)}), bf16[4,16,2048]{2,1,0:T(8,128)(2,1)S(1)}, u32[]{:S(2)}, u32[]{:S(2)}) async-start(bf16[4,16,2048]{2,1,0:T(8,128)(2,1)} %bitcast.1), calls=%async_computation | async-start | bytes 524288 | tf_op jit(solution)/shard_map/all_to_all | solution.py:74
Sparse Core Ops, SparseCore 0:
  9.5 37.1 all-gather.1
where the time goes:
time: 85.1 us; the launch traced here: 84.7 us
  waiting for transfers between devices  32.2 us (38%)
  between operations  14.8 us (17%)
  matrix products  12.2 us (14%)
  blocking collectives  9.92 us (12%)
  starting transfers between devices  8.1 us (10%)
  local copies, waits for them, and re-layouts  4.98 us (6%)
  other arithmetic  2.55 us (3%)
    all_gather x1, waiting for transfers between devices, local(): portion = lax.all_gather(draft_features, 'head', axis=1, tiled=True)  22.4 us
    unnamed x1, blocking collectives  9.92 us
    all_to_all x1, waiting for transfers between devices, local(): lax.all_to_all(key_send, 'seq', split_axis=0, concat_axis=0, tiled=True)  5.69 us
    dot_general x1, matrix products, local(): value_sum = jnp.dot(portion, w_value, preferred_element_type=jnp.float32)  4.71 us
    dot_general x1, matrix products, local(): key_sum = jnp.dot(portion, w_key, preferred_element_type=jnp.float32)  4.71 us
    all_to_all x1, starting transfers between devices, local(): lax.all_to_all(value_send, 'seq', split_axis=0, concat_axis=0, tiled=True)  4.65 us
    unnamed x8, local copies, waits for them, and re-layouts  4.49 us
    all_to_all x1, waiting for transfers between devices, local(): lax.all_to_all(value_send, 'seq', split_axis=0, concat_axis=0, tiled=True)  3.47 us
  transfers between devices with their start and end apart: 3, of which 3 were waited for; matrix products, arithmetic and copies ran while one was open for 15% of the time, Pallas kernels for 0%

commit v1 on v0

--- a/solution.py
+++ b/solution.py
@@ -57,7 +57,12 @@
         lax.all_gather(page_slot, "seq", axis=0, tiled=True),
     )
     placing = placement(all_owner, all_page, owner_self, req_dev, slot_cap, seq_count)
-    portion = lax.all_gather(draft_features, "head", axis=1, tiled=True)
+    ring = [draft_features]
+    for hop in range(3):
+        ring.append(lax.ppermute(ring[-1], "head", [(dev, (dev + 1) % 4) for dev in range(4)]))
+    portion = jnp.roll(
+        jnp.concatenate(ring[::-1], axis=1), (lax.axis_index("head") + 1) * ring[0].shape[1], axis=1
+    )
     key_sum = jnp.dot(portion, w_key, preferred_element_type=jnp.float32)
     value_sum = jnp.dot(portion, w_value, preferred_element_type=jnp.float32)
     key_local = jnp.where(

time: 85.1 us -> 80.7 us (0.948)
  between operations: 14.8 us -> 1.46 us
  local copies, waits for them, and re-layouts: 4.98 us -> 12.7 us
  waiting for transfers between devices: 32.2 us -> 37.6 us
  matrix products: 12.2 us -> 8.73 us
    ppermute x0 -> x3, waiting for transfers between devices: none -> 28.8 us  [local(): lax.ppermute(ring[-1], 'head', [(dev, (dev + 1) % 4) for dev in range(4)])]
    all_gather x1 -> x0, waiting for transfers between devices: 22.4 us -> none  [local(): portion = lax.all_gather(draft_features, 'head', axis=1, tiled=True)]
    unnamed x8 -> x21, local copies, waits for them, and re-layouts: 4.49 us -> 12.2 us
    dot_general x1, matrix products: 4.71 us -> 1.24 us  [local(): value_sum = jnp.dot(portion, w_value, preferred_element_type=jnp.float32)]
  transfers between devices with their start and end apart: 3 -> 5, of which waited for: 3 -> 4; matrix products, arithmetic and copies ran while one was open for 15% -> 16% of each run, Pallas kernels for 0% -> 0%
where the time goes in v1:
time: 80.7 us; the launch traced here: 80.3 us
  waiting for transfers between devices  37.6 us (47%)
  local copies, waits for them, and re-layouts  12.7 us (16%)
  blocking collectives  9.24 us (11%)
  matrix products  8.73 us (11%)
  starting transfers between devices  8 us (10%)
  other arithmetic  2.55 us (3%)
  between operations  1.46 us (2%)
    ppermute x3, waiting for transfers between devices, local(): lax.ppermute(ring[-1], 'head', [(dev, (dev + 1) % 4) for dev in range(4)])  28.8 us
    unnamed x21, local copies, waits for them, and re-layouts  12.2 us
    unnamed x1, blocking collectives  9.24 us
    all_to_all x1, waiting for transfers between devices, local(): lax.all_to_all(key_send, 'seq', split_axis=0, concat_axis=0, tiled=True)  5.76 us
    dot_general x1, matrix products, local(): key_sum = jnp.dot(portion, w_key, preferred_element_type=jnp.float32)  4.71 us
    all_to_all x1, starting transfers between devices, local(): lax.all_to_all(value_send, 'seq', split_axis=0, concat_axis=0, tiled=True)  4.02 us
    all_to_all x1, starting transfers between devices, local(): lax.all_to_all(key_send, 'seq', split_axis=0, concat_axis=0, tiled=True)  3.41 us
    all_to_all x1, waiting for transfers between devices, local(): lax.all_to_all(value_send, 'seq', split_axis=0, concat_axis=0, tiled=True)  3 us
  transfers between devices with their start and end apart: 5, of which 4 were waited for; matrix products, arithmetic and copies ran while one was open for 16% of the time, Pallas kernels for 0%

profile of v1, /device:TPU:0, one launch (start us, length us, event | category | flops | bytes accessed | tf_op | source)
XLA Modules:
  0.0 80.3 jit_solution(674749974030584863)
XLA Ops:
  0.6 0.0 copy-start
  0.6 0.5 collective-permute-start
  1.2 14.6 %collective-permute-done = bf16[256,2048]{1,0:T(8,128)(2,1)S(1)} collective-permute-done((bf16[256,2048]{1,0:T(8,128)(2,1)}, bf16[256,2048]{1,0:T(8,128)(2,1)S(1)}, u32[]{:S(2)}, u32[]{:S(2)}) %collective-permute-start) | collective-permute-done | bytes 1048608 | tf_op jit(solution)/shard_map/ppermute | solution.py:62
  15.8 0.0 collective-permute-start.1
  15.8 14.2 %collective-permute-done.1 = bf16[256,2048]{1,0:T(8,128)(2,1)S(1)} collective-permute-done((bf16[256,2048]{1,0:T(8,128)(2,1)S(1)}, bf16[256,2048]{1,0:T(8,128)(2,1)S(1)}, u32[]{:S(2)}, u32[]{:S(2)}) %collective-permute-start.1) | collective-permute-done | bytes 1048608 | tf_op jit(solution)/shard_map/ppermute | solution.py:62
  30.0 0.0 collective-permute-start.2
  30.0 0.7 iota_compare_fusion.4
  30.8 0.1 broadcast_in_dim.53
  30.9 1.2 %dynamic-slice = u32[1]{0:T(128)} dynamic-slice(u32[32]{0:T(128)} %constant.44, u32[]{:T(128)S(6)} %add.29), dynamic_slice_sizes={1} | dynamic-slice | bytes 12
  32.8 0.9 %dynamic-update-slice = s32[128]{0:T(128)S(1)} dynamic-update-slice(s32[128]{0:T(128)S(1)} %broadcast.32.clone, s32[32]{0:T(128)} %param.10, u32[]{:T(128)} %bitcast) | dynamic-update-slice | bytes 260
  33.7 0.8 %dynamic-update-slice.1 = s32[128]{0:T(128)S(1)} dynamic-update-slice(s32[128]{0:T(128)S(1)} %broadcast.32.clone.1, s32[32]{0:T(128)} %param.11, u32[]{:T(128)} %bitcast) | dynamic-update-slice | bytes 260
  34.5 9.2 %all-reduce.2 = (s32[128]{0:T(128)S(1)}, s32[128]{0:T(128)S(1)}) all-reduce(s32[128]{0:T(128)S(1)} %dynamic-update-slice, s32[128]{0:T(128)S(1)} %dynamic-update-slice.1), channel_id=1, replica_groups=mesh['grp'=2,'seq'=4,'head'=4] {'seq'}, use_global_device_ids=true, to_apply=%add | all-reduce | flops 256 | bytes 2048
  43.8 0.1 eq.69
  43.9 0.2 select_reduce_fusion
  44.1 0.1 reduce_sum.21
  44.2 0.1 mul.22
  44.3 0.9 %select_reduce_fusion.1 = s32[32]{0:T(128)S(1)} fusion(s32[32]{0:T(128)} %param.10), kind=kLoop, calls=%fused_computation.28 | loop fusion | flops 5088 | bytes 256 | tf_op jit(solution)/shard_map/reduce_sum | solution.py:13
  45.2 0.7 multiply_add_fusion
  45.9 0.0 copy-start.2
  45.9 0.0 collective-permute-done.2
  45.9 1.4 %constant_dynamic-update-slice_fusion.7 = bf16[256,16384]{1,0:T(8,128)(2,1)S(1)} fusion(bf16[256,2048]{1,0:T(8,128)(2,1)} %collective-permute-done.2), kind=kLoop, calls=%fused_computation.25 | loop fusion | bytes 2097152
  47.3 0.1 constant_dynamic-update-slice_fusion.6
  47.4 0.1 constant_dynamic-update-slice_fusion.5
  47.5 1.3 %constant_dynamic-update-slice_fusion.4 = bf16[256,16384]{1,0:T(8,128)(2,1)S(1)} fusion(bf16[256,16384]{1,0:T(8,128)(2,1)S(1)} %constant_dynamic-update-slice_fusion.5, bf16[256,2048]{1,0:T(8,128)(2,1)} %param.6), kind=kLoop, calls=%fused_computation.22 | loop fusion | bytes 2097152
  48.8 1.3 %constant_dynamic-update-slice_fusion.3 = bf16[256,16384]{1,0:T(8,128)(2,1)S(1)} fusion(bf16[256,16384]{1,0:T(8,128)(2,1)S(1)} %constant_dynamic-update-slice_fusion.4, bf16[256,2048]{1,0:T(8,128)(2,1)} %collective-permute-done.2), kind=kLoop, calls=%fused_computation.21 | loop fusion | bytes 2097152
  50.1 0.1 constant_dynamic-update-slice_fusion.2
  50.2 0.1 constant_dynamic-update-slice_fusion.1
  50.3 0.0 copy-done
  50.4 0.1 constant_dynamic-update-slice_fusion
  50.5 0.0 copy-start.1
  50.5 3.2 %copy-done.1 = bf16[256,16384]{1,0:T(8,128)(2,1)} copy-done((bf16[256,16384]{1,0:T(8,128)(2,1)}, bf16[256,16384]{1,0:T(8,128)(2,1)S(1)}, u32[]{:S(2)}) %copy-start.1) | copy-done | bytes 8388632
  53.7 0.0 copy-done.2
  53.7 1.2 %fusion = bf16[256,256]{1,0:T(8,128)(2,1)S(1)} fusion(bf16[8192,256]{1,0:T(8,128)(2,1)S(1)} %copy-done.2, bf16[256,16384]{1,0:T(8,128)(2,1)S(1)} %constant_dynamic-update-slice_fusion, s32[]{:T(128)S(6)} %select_n.38), kind=kOutput, calls=%fused_computation | convolution fusion | flops 1073741824 | bytes 8519684 | tf_op jit(solution)/shard_map/dot_general | solution.py:67
  54.9 0.1 reshape.67
  55.0 1.0 %convolution_convert_fusion.1 = bf16[64,2048]{1,0:T(8,128)(2,1)} fusion(pred[32,2048]{1,0:T(8,128)(4,1)S(1)} %bitcast.21, bf16[32,2048]{1,0:T(8,128)(2,1)S(1)} %reshape.67, s32[32]{0:T(128)S(1)} %multiply_add_fusion), kind=kOutput, calls=%fused_computation.5 | convolution fusion | flops 8587264 | bytes 458880 | tf_op jit(solution)/shard_map/dot_general | solution.py:25
  56.1 4.0 %all-to-all-start.1 = ((bf16[4,16,2048]{2,1,0:T(8,128)(2,1)}), bf16[4,16,2048]{2,1,0:T(8,128)(2,1)S(1)}, u32[]{:S(2)}, u32[]{:S(2)}) async-start(bf16[4,16,2048]{2,1,0:T(8,128)(2,1)} %bitcast.3), calls=%async_computation.1 | async-start | bytes 524288 | tf_op jit(solution)/shard_map/all_to_all | solution.py:80
  60.1 4.7 %fusion.2 = bf16[256,256]{1,0:T(8,128)(2,1)S(1)} fusion(bf16[8192,256]{1,0:T(8,128)(2,1)} %param.7, bf16[256,16384]{1,0:T(8,128)(2,1)} %copy-done.1, s32[]{:T(128)S(6)} %select_n.38), kind=kOutput, calls=%fused_computation.2 | convolution fusion | flops 1073741824 | bytes 8519684 | tf_op jit(solution)/shard_map/dot_general | solution.py:66
  64.8 0.1 reshape.65
  64.9 1.0 %convolution_convert_fusion.3 = bf16[64,2048]{1,0:T(8,128)(2,1)} fusion(pred[32,2048]{1,0:T(8,128)(4,1)S(1)} %bitcast.22, bf16[32,2048]{1,0:T(8,128)(2,1)S(1)} %reshape.65, s32[32]{0:T(128)S(1)} %multiply_add_fusion), kind=kOutput, calls=%fused_computation.7 | convolution fusion | flops 8587264 | bytes 458880 | tf_op jit(solution)/shard_map/dot_general | solution.py:25
  65.9 3.0 %all-to-all-done.1 = bf16[4,16,2048]{2,1,0:T(8,128)(2,1)S(1)} async-done(((bf16[4,16,2048]{2,1,0:T(8,128)(2,1)}), bf16[4,16,2048]{2,1,0:T(8,128)(2,1)S(1)}, u32[]{:S(2)}, u32[]{:S(2)}) %all-to-all-start.1) | async-done | bytes 262176 | tf_op jit(solution)/shard_map/all_to_all | solution.py:80
  68.9 3.4 %all-to-all-start = ((bf16[4,16,2048]{2,1,0:T(8,128)(2,1)}), bf16[4,16,2048]{2,1,0:T(8,128)(2,1)S(1)}, u32[]{:S(2)}, u32[]{:S(2)}) async-start(bf16[4,16,2048]{2,1,0:T(8,128)(2,1)} %bitcast.1), calls=%async_computation | async-start | bytes 524288 | tf_op jit(solution)/shard_map/all_to_all | solution.py:79
  72.3 0.3 convolution_convert_fusion.4
  72.6 0.2 convolution_convert_fusion
  72.8 0.8 copy.10
  73.6 5.8 %all-to-all-done = bf16[4,16,2048]{2,1,0:T(8,128)(2,1)S(1)} async-done(((bf16[4,16,2048]{2,1,0:T(8,128)(2,1)}), bf16[4,16,2048]{2,1,0:T(8,128)(2,1)S(1)}, u32[]{:S(2)}, u32[]{:S(2)}) %all-to-all-start) | async-done | bytes 262176 | tf_op jit(solution)/shard_map/all_to_all | solution.py:79
  79.3 0.2 convolution_convert_fusion.2
  79.6 0.8 copy.9
  (6 shorter events, 0.1 us)
Async XLA Ops:
  0.6 49.7 %copy-start = (bf16[256,2048]{1,0:T(8,128)(2,1)S(1)}, bf16[256,2048]{1,0:T(8,128)(2,1)}, u32[]{:S(2)}) copy-start(bf16[256,2048]{1,0:T(8,128)(2,1)} %param.6) | copy-start | bytes 3145732
  0.6 15.2 %collective-permute-start = (bf16[256,2048]{1,0:T(8,128)(2,1)}, bf16[256,2048]{1,0:T(8,128)(2,1)S(1)}, u32[]{:S(2)}, u32[]{:S(2)}) collective-permute-start(bf16[256,2048]{1,0:T(8,128)(2,1)} %param.6), channel_id=1, source_target_pairs={{0,1},{1,2},{2,3},{3,0},{4,5},{5,6},{6,7},{7,4},{8,9},{9,10},{10,1... | collective-permute-start | bytes 3145736 | tf_op jit(solution)/shard_map/ppermute | solution.py:62
  15.8 14.2 %collective-permute-start.1 = (bf16[256,2048]{1,0:T(8,128)(2,1)S(1)}, bf16[256,2048]{1,0:T(8,128)(2,1)S(1)}, u32[]{:S(2)}, u32[]{:S(2)}) collective-permute-start(bf16[256,2048]{1,0:T(8,128)(2,1)S(1)} %collective-permute-done), channel_id=1, source_target_pairs={{0,1},{1,2},{2,3},{3,0},{4,5},{5,6},{6,7},{7,4},{8,9},{9,10},{10,1... | collective-permute-start | bytes 3145736 | tf_op jit(solution)/shard_map/ppermute | solution.py:62
  30.0 15.8 %collective-permute-start.2 = (bf16[256,2048]{1,0:T(8,128)(2,1)S(1)}, bf16[256,2048]{1,0:T(8,128)(2,1)}, u32[]{:S(2)}, u32[]{:S(2)}) collective-permute-start(bf16[256,2048]{1,0:T(8,128)(2,1)S(1)} %collective-permute-done.1), channel_id=1, source_target_pairs={{0,1},{1,2},{2,3},{3,0},{4,5},{5,6},{6,7},{7,4},{8,9},{9,10},{10,1... | collective-permute-start | bytes 3145736 | tf_op jit(solution)/shard_map/ppermute | solution.py:62
  45.9 7.8 %copy-start.2 = (bf16[8192,256]{1,0:T(8,128)(2,1)S(1)}, bf16[8192,256]{1,0:T(8,128)(2,1)}, u32[]{:S(2)}) copy-start(bf16[8192,256]{1,0:T(8,128)(2,1)} %param.8) | copy-start | bytes 12582916
  50.5 3.2 %copy-start.1 = (bf16[256,16384]{1,0:T(8,128)(2,1)}, bf16[256,16384]{1,0:T(8,128)(2,1)S(1)}, u32[]{:S(2)}) copy-start(bf16[256,16384]{1,0:T(8,128)(2,1)S(1)} %constant_dynamic-update-slice_fusion) | copy-start | bytes 25165828
  56.1 12.8 %all-to-all-start.1 = ((bf16[4,16,2048]{2,1,0:T(8,128)(2,1)}), bf16[4,16,2048]{2,1,0:T(8,128)(2,1)S(1)}, u32[]{:S(2)}, u32[]{:S(2)}) async-start(bf16[4,16,2048]{2,1,0:T(8,128)(2,1)} %bitcast.3), calls=%async_computation.1 | async-start | bytes 524288 | tf_op jit(solution)/shard_map/all_to_all | solution.py:80
  68.9 10.4 %all-to-all-start = ((bf16[4,16,2048]{2,1,0:T(8,128)(2,1)}), bf16[4,16,2048]{2,1,0:T(8,128)(2,1)S(1)}, u32[]{:S(2)}, u32[]{:S(2)}) async-start(bf16[4,16,2048]{2,1,0:T(8,128)(2,1)} %bitcast.1), calls=%async_computation | async-start | bytes 524288 | tf_op jit(solution)/shard_map/all_to_all | solution.py:79
